TPU v7x, 128 devices: a whole 4x4x4 slice. The times are simulated.
128 devices in a mesh: pr: 16 (over z_lo, y, core), pc: 8 (over z_hi, x).
Axes of the slice: x: 4, y: 4, z: 4 (z_hi: 2, z_lo: 2; z = z_hi * 2 + z_lo), core: 2. Of those that a mesh axis runs over, the one named last changes fastest.
Arguments:
- pair_array: bfloat16 [1024, 1024, 128], P('pr', 'pc'), may hold values from -6 to 6
- left_weight: bfloat16 [128, 128], replicated, may hold values from -0.5 to 0.5
- right_weight: bfloat16 [128, 128], replicated, may hold values from -0.5 to 0.5
- left_gate: bfloat16 [128, 128], replicated, may hold values from -0.5 to 0.5
- right_gate: bfloat16 [128, 128], replicated, may hold values from -0.5 to 0.5
- mid_gain: float32 [128], replicated, may hold values from 0.25 to 1.75
- out_weight: bfloat16 [128, 128], replicated, may hold values from -0.5 to 0.5
- out_gate: bfloat16 [128, 128], replicated, may hold values from -0.5 to 0.5
Outputs:
- pair_update: bfloat16 [1024, 1024, 128], P('pr', 'pc')
All inputs are finite; a program needn't handle non-finite values.
Results may differ from a plain program's by a relative error of at most 0.012.
Values may be sent and summed in bfloat16 or wider, within the bound.
A program may use at most 128 MiB of HBM per device.

v0:
```python
import jax
import jax.numpy as jnp
from jax import lax
from jax.sharding import PartitionSpec as P


def unit_channels(values, channel_gain):
    centred = values - jnp.mean(values, axis=-1, keepdims=True)
    return (
        centred
        * lax.rsqrt(jnp.mean(centred * centred, axis=-1, keepdims=True) + 1e-05)
        * channel_gain
    )


def make_factors(pair_in, left_weight, right_weight, left_gate, right_gate):
    left = jnp.einsum("ijc,cd->ijd", pair_in, left_weight, preferred_element_type=jnp.float32)
    left = left * jax.nn.sigmoid(
        jnp.einsum("ijc,cd->ijd", pair_in, left_gate, preferred_element_type=jnp.float32)
    )
    right = jnp.einsum("ijc,cd->ijd", pair_in, right_weight, preferred_element_type=jnp.float32)
    right = right * jax.nn.sigmoid(
        jnp.einsum("ijc,cd->ijd", pair_in, right_gate, preferred_element_type=jnp.float32)
    )
    return (pair_in, left.astype(jnp.bfloat16), right.astype(jnp.bfloat16))


def to_pair(mixed, ready, mid_gain, out_weight, out_gate):
    scaled = unit_channels(mixed.astype(jnp.float32), mid_gain).astype(jnp.bfloat16)
    scaled = lax.optimization_barrier(scaled)
    gate = jax.nn.sigmoid(
        jnp.einsum("ijc,cd->ijd", ready, out_gate, preferred_element_type=jnp.float32)
    )
    return (
        jnp.einsum("ijd,dc->ijc", scaled, out_weight, preferred_element_type=jnp.float32) * gate
    ).astype(jnp.bfloat16)


def on_device(
    pair_array, left_weight, right_weight, left_gate, right_gate, mid_gain, out_weight, out_gate
):
    ready, left, right = make_factors(pair_array, left_weight, right_weight, left_gate, right_gate)
    count = pair_array.shape[0] * lax.axis_size("pr")
    left_lines, right_lines = (
        lax.all_to_all(left, "pr", split_axis=2, concat_axis=0, tiled=True),
        lax.all_to_all(right, "pr", split_axis=2, concat_axis=0, tiled=True),
    )
    strip = jnp.einsum(
        "kid,kjd->ijd",
        lax.all_gather(left_lines, "pc", axis=1, tiled=True),
        right_lines,
        preferred_element_type=jnp.float32,
    )
    strip = (strip * count ** (-0.5)).astype(jnp.bfloat16)
    mixed = lax.all_to_all(strip, "pr", split_axis=0, concat_axis=2, tiled=True)
    return to_pair(mixed, ready, mid_gain, out_weight, out_gate)


def solution(mesh):
    return jax.shard_map(
        on_device,
        mesh=mesh,
        in_specs=(P("pr", "pc", None), P(), P(), P(), P(), P(), P(), P()),
        out_specs=P("pr", "pc", None),
        check_vma=False,
    )
```

profile of v0, /device:TPU:1, one launch (start us, length us, event | category | flops | bytes accessed | tf_op | source)
XLA Modules:
  0.0 335.6 jit_solution(2353364457748067482)
XLA Ops:
  6.5 1.6 copy-done
  8.1 1.4 fusion.12
  9.6 2.6 multiply_convert_fusion.2
  12.2 4.2 %copy.24 = bf16[64,128,128]{1,0,2:T(8,128)(2,1)} copy(bf16[64,128,128]{2,1,0:T(8,128)(2,1)} %multiply_convert_fusion.2) | data formatting | bytes 4194304 | tf_op jit(solution)/shard_map/convert_element_type | solution.py:25
  16.4 33.7 %all_to_all.45 = bf16[64,128,128]{1,0,2:T(8,128)(2,1)S(1)} all-to-all(bf16[64,128,128]{1,0,2:T(8,128)(2,1)} %copy.24), channel_id=1, replica_groups=mesh['pr'=16,'pc'=8] {'pr'}, dimensions={2} | all-to-all | bytes 4194304 | tf_op jit(solution)/shard_map/all_to_all | solution.py:45
  50.0 1.5 copy.26
  51.5 0.0 all-gather.2.cloned.1.call-update
  51.6 0.7 fusion.15
  52.2 0.0 copy-done.5
  52.3 2.6 multiply_convert_fusion.3
  54.9 4.2 %copy.21 = bf16[64,128,128]{1,0,2:T(8,128)(2,1)} copy(bf16[64,128,128]{2,1,0:T(8,128)(2,1)} %multiply_convert_fusion.3) | data formatting | bytes 4194304 | tf_op jit(solution)/shard_map/convert_element_type | solution.py:25
  59.1 36.1 %all_to_all.46 = bf16[64,128,128]{1,0,2:T(8,128)(2,1)S(1)} all-to-all(bf16[64,128,128]{1,0,2:T(8,128)(2,1)} %copy.21), channel_id=1, replica_groups=mesh['pr'=16,'pc'=8] {'pr'}, dimensions={2} | all-to-all | bytes 4194304 | tf_op jit(solution)/shard_map/all_to_all | solution.py:46
  95.2 3.1 copy.23
  98.3 177.9 %all-gather.2.cloned.1.call-done = bf16[1024,1024,8]{1,0,2:T(8,128)(2,1)} async-done(((bf16[1024,128,8]{1,0,2:T(8,128)(2,1)}), bf16[1024,1024,8]{1,0,2:T(8,128)(2,1)}) %all-gather.2.cloned.1.call-update) | async-done | bytes 16777232 | tf_op jit(solution)/shard_map/all_gather | solution.py:50
  276.2 10.3 %fusion.5 = bf16[1024,128,8]{0,1,2:T(8,128)(2,1)} fusion(bf16[1024,1024,8]{1,0,2:T(8,128)(2,1)} %all-gather.2.cloned.1.call-done, bf16[1024,128,8]{1,2,0:T(8,128)(2,1)} %bitcast.56), kind=kOutput, calls=%fused_computation.12 | convolution fusion | flops 2149580800 | bytes 20971520 | tf_op jit(solution)/shard_map/kid,kjd->ijd/dot_general | solution.py:48
  286.5 4.1 %copy.28 = bf16[1024,128,8]{1,2,0:T(8,128)(2,1)} copy(bf16[1024,128,8]{0,1,2:T(8,128)(2,1)} %fusion.5) | data formatting | bytes 4194304 | tf_op jit(solution)/shard_map/convert_element_type | solution.py:54
  290.6 32.9 %all_to_all.47 = bf16[1024,128,8]{1,2,0:T(8,128)(2,1)S(1)} all-to-all(bf16[1024,128,8]{1,2,0:T(8,128)(2,1)} %copy.28), channel_id=1, replica_groups=mesh['pr'=16,'pc'=8] {'pr'}, dimensions={0} | all-to-all | bytes 4194304 | tf_op jit(solution)/shard_map/all_to_all | solution.py:55
  323.5 0.3 fusion.3
  323.8 0.6 multiply_reduce_fusion
  324.5 0.9 fusion.2
  325.4 0.0 copy-start.6
  325.4 0.7 fusion.9
  326.1 0.0 copy-done.6
  326.1 2.6 multiply_convert_fusion
  (13 shorter events, 0.0 us)
Async XLA Ops:
  6.5 1.6 copy-start
  6.5 3.0 copy-start.4
  6.5 269.6 %all-gather.2.cloned.1.call-start = ((), (), s32[]{:S(2)}) async-start(), calls=%async_computation.3 | async-start | bytes 18874368 | tf_op jit(solution)/shard_map/all_gather | solution.py:50
  50.0 1.5 copy-start.1
  51.5 0.8 copy-start.5
  290.6 33.9 %copy-start.3 = (f32[128]{0:T(128)S(1)}, f32[128]{0:T(128)}, u32[]{:S(2)}) copy-start(f32[128]{0:T(128)} %param.13) | copy-start | bytes 1540
  323.5 1.9 copy-start.2
  325.4 0.8 copy-start.6
Sparse Core Ops, SparseCore 0:
  51.7 224.4 all-gather.1
where the time goes:
time: 336 us
  waiting for transfers between devices  178 us (53%)
  blocking collectives  103 us (31%)
  matrix products  21 us (6%)
  local copies, waits for them, and re-layouts  18.7 us (6%)
  between operations  13.5 us (4%)
    all_gather x1, waiting for transfers between devices, on_device(): lax.all_gather(left_lines, 'pc', axis=1, tiled=True)  178 us
    all_to_all x1, blocking collectives, on_device(): lax.all_to_all(right, 'pr', split_axis=2, concat_axis=0, tiled=True)  36.1 us
    all_to_all x1, blocking collectives, on_device(): lax.all_to_all(left, 'pr', split_axis=2, concat_axis=0, tiled=True)  33.7 us
    all_to_all x1, blocking collectives, on_device(): mixed = lax.all_to_all(strip, 'pr', split_axis=0, concat_axis=2, tiled=True)  32.9 us
    dot_general x1, matrix products, on_device(): jnp.einsum('kid,kjd->ijd', lax.all_gather(left_lines, 'pc', axis=1, tiled...  10.3 us
    convert_element_type x2, local copies, waits for them, and re-layouts, make_factors(): return (pair_in, left.astype(jnp.bfloat16), right.astype(jnp.bfloat16))  8.31 us
  transfers between devices with their start and end apart: 1, of which 1 were waited for; matrix products, arithmetic and copies ran while one was open for 3% of the time, Pallas kernels for 0%

commit v1 on v0

v1 whole, which is shorter than its diff:
```python
import jax
import jax.numpy as jnp
from jax import lax
from jax.sharding import PartitionSpec as P

BOTH = ("pr", "pc")


def factor(pair_in, weight, gate):
    value = jnp.einsum("ijc,cd->ijd", pair_in, weight, preferred_element_type=jnp.float32)
    value = value * jax.nn.sigmoid(
        jnp.einsum("ijc,cd->ijd", pair_in, gate, preferred_element_type=jnp.float32)
    )
    return value.astype(jnp.bfloat16)


def on_device(
    pair_array, left_weight, right_weight, left_gate, right_gate, mid_gain, out_weight, out_gate
):
    rows, columns, _ = pair_array.shape
    pr, pc = lax.axis_size("pr"), lax.axis_size("pc")
    count = rows * pr
    left = factor(pair_array, left_weight, left_gate)
    right = factor(pair_array, right_weight, right_gate)
    left = lax.all_to_all(jnp.moveaxis(left, 2, 0), BOTH, split_axis=0, concat_axis=0, tiled=True)
    right = lax.all_to_all(jnp.moveaxis(right, 2, 0), BOTH, split_axis=0, concat_axis=0, tiled=True)
    left = left.reshape(pr, pc, rows, columns)
    right = right.reshape(pr, pc, rows, columns)
    left = jnp.moveaxis(left, 1, 2).reshape(count, count)
    right = jnp.moveaxis(right, 1, 2).reshape(count, count)
    mixed = jnp.einsum("ki,kj->ij", left, right, preferred_element_type=jnp.float32)
    mixed = (mixed * count ** (-0.5)).astype(jnp.bfloat16)
    mixed = jnp.moveaxis(mixed.reshape(pr, rows, pc, columns), 2, 1).reshape(pr * pc, rows, columns)
    mixed = lax.all_to_all(mixed, BOTH, split_axis=0, concat_axis=0, tiled=True)
    values = mixed.astype(jnp.float32)
    centred = values - jnp.mean(values, axis=0, keepdims=True)
    scaled = (
        centred
        * lax.rsqrt(jnp.mean(centred * centred, axis=0, keepdims=True) + 1e-05)
        * mid_gain[:, None, None]
    ).astype(jnp.bfloat16)
    gate = jax.nn.sigmoid(
        jnp.einsum("ijc,cd->ijd", pair_array, out_gate, preferred_element_type=jnp.float32)
    )
    return (
        jnp.einsum("dij,dc->ijc", scaled, out_weight, preferred_element_type=jnp.float32) * gate
    ).astype(jnp.bfloat16)


def solution(mesh):
    return jax.shard_map(
        on_device,
        mesh=mesh,
        in_specs=(P("pr", "pc", None), P(), P(), P(), P(), P(), P(), P()),
        out_specs=P("pr", "pc", None),
        check_vma=False,
    )
```

time: 336 us -> 132 us (0.39)
  waiting for transfers between devices: 178 us -> 48 us
  blocking collectives: 103 us -> 34.5 us
  starting transfers between devices: 0.01 us -> 18 us
  between operations: 13.5 us -> 0.14 us
  matrix products: 21 us -> 12.4 us
    all_gather x1 -> x0, waiting for transfers between devices: 178 us -> none  [on_device(): lax.all_gather(left_lines, 'pc', axis=1, tiled=True)]
    all_to_all x3 -> x1, blocking collectives: 103 us -> 34.5 us  [on_device(): mixed = lax.all_to_all(mixed, BOTH, split_axis=0, concat_axis=0, tiled=True)]
    all_to_all x0 -> x2, waiting for transfers between devices: none -> 48 us  [the longest x1 24 us: on_device(): lax.all_to_all(jnp.moveaxis(right, 2, 0), BOTH, split_axis=0, concat_axis...]
    all_to_all x0 -> x2, starting transfers between devices: none -> 18 us  [the longest x1 11.9 us: on_device(): lax.all_to_all(jnp.moveaxis(left, 2, 0), BOTH, split_axis=0, concat_axis=...]
    reshape x0 -> x3, local copies, waits for them, and re-layouts: none -> 8.8 us  [the longest x1 4.67 us: on_device(): left = left.reshape(pr, pc, rows, columns)]
    dot_general x7, matrix products: 21 us -> 12.4 us  [the longest x2 2.67 us: factor(): jnp.einsum('ijc,cd->ijd', pair_in, gate, preferred_element_type=jnp.float32)]
    convert_element_type x3 -> x2, local copies, waits for them, and re-layouts: 12.4 us -> 5.34 us  [factor(): return value.astype(jnp.bfloat16)]
    all_to_all x2 -> x0, local copies, waits for them, and re-layouts: 4.62 us -> none  [the longest x1 3.13 us: on_device(): lax.all_to_all(right, 'pr', split_axis=2, concat_axis=0, tiled=True)]
  transfers between devices with their start and end apart: 1 -> 2, of which waited for: 1 -> 2; matrix products, arithmetic and copies ran while one was open for 3% -> 7% of each run, Pallas kernels for 0% -> 0%
where the time goes in v1:
time: 132 us; the launch traced here: 131 us
  waiting for transfers between devices  48 us (36%)
  blocking collectives  34.5 us (26%)
  starting transfers between devices  18 us (14%)
  local copies, waits for them, and re-layouts  16.4 us (12%)
  matrix products  12.4 us (9%)
  other arithmetic  1.68 us (1%)
    all_to_all x1, blocking collectives, on_device(): mixed = lax.all_to_all(mixed, BOTH, split_axis=0, concat_axis=0, tiled=True)  34.5 us
    all_to_all x1, waiting for transfers between devices, on_device(): lax.all_to_all(jnp.moveaxis(right, 2, 0), BOTH, split_axis=0, concat_axis...  24 us
    all_to_all x1, waiting for transfers between devices, on_device(): lax.all_to_all(jnp.moveaxis(left, 2, 0), BOTH, split_axis=0, concat_axis=...  23.9 us
    all_to_all x1, starting transfers between devices, on_device(): lax.all_to_all(jnp.moveaxis(left, 2, 0), BOTH, split_axis=0, concat_axis=...  11.9 us
    all_to_all x1, starting transfers between devices, on_device(): lax.all_to_all(jnp.moveaxis(right, 2, 0), BOTH, split_axis=0, concat_axis...  6.06 us
    convert_element_type x2, local copies, waits for them, and re-layouts, factor(): return value.astype(jnp.bfloat16)  5.34 us
    reshape x1, local copies, waits for them, and re-layouts, on_device(): left = left.reshape(pr, pc, rows, columns)  4.67 us
    reshape x1, local copies, waits for them, and re-layouts, on_device(): right = right.reshape(pr, pc, rows, columns)  3.51 us
  transfers between devices with their start and end apart: 2, of which 2 were waited for; matrix products, arithmetic and copies ran while one was open for 7% of the time, Pallas kernels for 0%

profile of v1, /device:TPU:1, one launch (start us, length us, event | category | flops | bytes accessed | tf_op | source)
XLA Modules:
  0.0 131.1 jit_solution(14817033417181162376)
XLA Ops:
  0.0 1.6 %copy-done = bf16[64,128,128]{2,1,0:T(8,128)(2,1)S(1)} copy-done((bf16[64,128,128]{2,1,0:T(8,128)(2,1)S(1)}, bf16[64,128,128]{2,1,0:T(8,128)(2,1)}, u32[]{:S(2)}) %copy-start) | copy-done | bytes 2097176
  1.6 1.5 %fusion.22 = f32[128,64,128]{2,0,1:T(8,128)S(1)} fusion(bf16[64,128,128]{2,1,0:T(8,128)(2,1)S(1)} %copy-done, bf16[128,128]{1,0:T(8,128)(2,1)} %param.9), kind=kOutput, calls=%fused_computation.24 | convolution fusion | flops 268435456 | bytes 6324224 | tf_op jit(solution)/shard_map/ijc,cd->ijd/dot_general | solution.py:10
  3.1 1.3 %multiply_convert_fusion.3 = bf16[128,64,128]{2,0,1:T(8,128)(2,1)S(1)} fusion(f32[128,64,128]{2,0,1:T(8,128)S(1)} %fusion.22, bf16[64,128,128]{2,1,0:T(8,128)(2,1)S(1)} %copy-done, bf16[128,128]{1,0:T(8,128)(2,1)S(1)} %copy-done.5), kind=kOutput, calls=%fused_computation.10 | convolution fusion | flops 273678336 | bytes 8421376 | tf_op jit(solution)/shard_map/ijc,cd->ijd/dot_general | solution.py:12
  4.4 2.7 %copy.24 = bf16[128,64,128]{2,1,0:T(8,128)(2,1)} copy(bf16[128,64,128]{2,0,1:T(8,128)(2,1)S(1)} %multiply_convert_fusion.3) | data formatting | bytes 4194304 | tf_op jit(solution)/shard_map/convert_element_type | solution.py:14
  7.1 11.9 %all-to-all-start = ((bf16[128,64,128]{2,1,0:T(8,128)(2,1)}), bf16[128,64,128]{2,1,0:T(8,128)(2,1)}, u32[]{:S(2)}, u32[]{:S(2)}) async-start(bf16[128,64,128]{2,1,0:T(8,128)(2,1)} %copy.24), calls=%async_computation | async-start | bytes 4194304 | tf_op jit(solution)/shard_map/all_to_all | solution.py:25
  19.1 0.7 fusion.19
  19.8 0.0 copy-done.6
  19.8 1.3 %multiply_convert_fusion.2 = bf16[128,64,128]{2,0,1:T(8,128)(2,1)S(1)} fusion(f32[128,64,128]{2,0,1:T(8,128)S(1)} %fusion.19, bf16[64,128,128]{2,1,0:T(8,128)(2,1)S(1)} %copy-done, bf16[128,128]{1,0:T(8,128)(2,1)S(1)} %copy-done.6), kind=kOutput, calls=%fused_computation.9 | convolution fusion | flops 273678336 | bytes 8421376 | tf_op jit(solution)/shard_map/ijc,cd->ijd/dot_general | solution.py:12
  21.2 2.7 %copy.28 = bf16[128,64,128]{2,1,0:T(8,128)(2,1)} copy(bf16[128,64,128]{2,0,1:T(8,128)(2,1)S(1)} %multiply_convert_fusion.2) | data formatting | bytes 4194304 | tf_op jit(solution)/shard_map/convert_element_type | solution.py:14
  23.8 23.9 %all-to-all-done = bf16[128,64,128]{2,1,0:T(8,128)(2,1)} async-done(((bf16[128,64,128]{2,1,0:T(8,128)(2,1)}), bf16[128,64,128]{2,1,0:T(8,128)(2,1)}, u32[]{:S(2)}, u32[]{:S(2)}) %all-to-all-start) | async-done | bytes 2097184 | tf_op jit(solution)/shard_map/all_to_all | solution.py:25
  47.8 6.1 %all-to-all-start.1 = ((bf16[128,64,128]{2,1,0:T(8,128)(2,1)}), bf16[128,64,128]{2,1,0:T(8,128)(2,1)}, u32[]{:S(2)}, u32[]{:S(2)}) async-start(bf16[128,64,128]{2,1,0:T(8,128)(2,1)} %copy.28), calls=%async_computation.1 | async-start | bytes 4194304 | tf_op jit(solution)/shard_map/all_to_all | solution.py:26
  53.9 4.7 %copy.25 = bf16[16,8,64,128]{3,1,2,0:T(8,128)(2,1)} copy(bf16[16,8,64,128]{3,2,1,0:T(8,128)(2,1)} %bitcast.2) | data formatting | bytes 4194304 | tf_op jit(solution)/shard_map/reshape | solution.py:27
  58.5 24.0 %all-to-all-done.1 = bf16[128,64,128]{2,1,0:T(8,128)(2,1)} async-done(((bf16[128,64,128]{2,1,0:T(8,128)(2,1)}), bf16[128,64,128]{2,1,0:T(8,128)(2,1)}, u32[]{:S(2)}, u32[]{:S(2)}) %all-to-all-start.1) | async-done | bytes 2097184 | tf_op jit(solution)/shard_map/all_to_all | solution.py:26
  82.6 3.5 %copy.29 = bf16[16,8,64,128]{3,1,2,0:T(8,128)(2,1)S(1)} copy(bf16[16,8,64,128]{3,2,1,0:T(8,128)(2,1)} %bitcast.6) | data formatting | bytes 4194304 | tf_op jit(solution)/shard_map/reshape | solution.py:28
  86.1 2.4 %fusion.11 = bf16[128,8,8,128]{3,1,2,0:T(8,128)(2,1)S(1)} fusion(bf16[128,8,8,128]{3,2,1,0:T(8,128)(2,1)S(1)} %bitcast.51, bf16[128,8,8,128]{3,2,1,0:T(8,128)(2,1)S(1)} %bitcast.50), kind=kOutput, calls=%fused_computation.17 | convolution fusion | flops 2149580800 | bytes 6291456 | tf_op jit(solution)/shard_map/ki,kj->ij/dot_general | solution.py:31
  88.5 0.6 copy.42
  89.1 0.6 copy.30
  89.7 34.5 %all_to_all.15 = bf16[128,64,128]{2,1,0:T(8,128)(2,1)S(1)} all-to-all(bf16[128,64,128]{2,1,0:T(8,128)(2,1)S(1)} %bitcast.49), channel_id=1, replica_groups=mesh['pr'=16,'pc'=8] {'pr','pc'}, dimensions={0} | all-to-all | bytes 4194304 | tf_op jit(solution)/shard_map/all_to_all | solution.py:34
  124.2 0.4 convert_reduce_fusion
  124.6 0.6 fusion.2
  125.2 0.7 fusion.4
  125.9 0.0 copy-done.3
  126.0 2.5 %fusion.9 = f32[64,128,128]{2,1,0:T(8,128)S(1)} fusion(bf16[128,64,128]{2,1,0:T(8,128)(2,1)S(1)} %fusion.4, bf16[128,128]{1,0:T(8,128)(2,1)S(1)} %copy-done.3), kind=kOutput, calls=%fused_computation.15 | convolution fusion | flops 268435456 | bytes 6324224 | tf_op jit(solution)/shard_map/dij,dc->ijc/dot_general | solution.py:46
  128.5 2.6 %multiply_convert_fusion = bf16[64,128,128]{2,1,0:T(8,128)(2,1)} fusion(f32[64,128,128]{2,1,0:T(8,128)S(1)} %fusion.9, bf16[64,128,128]{2,1,0:T(8,128)(2,1)S(1)} %copy-done, bf16[128,128]{1,0:T(8,128)(2,1)S(1)} %copy-done.7), kind=kOutput, calls=%fused_computation.7 | convolution fusion | flops 273678336 | bytes 8421376 | tf_op jit(solution)/shard_map/ijc,cd->ijd/dot_general | solution.py:43
  (15 shorter events, 0.1 us)
Async XLA Ops:
  0.0 1.6 %copy-start = (bf16[64,128,128]{2,1,0:T(8,128)(2,1)S(1)}, bf16[64,128,128]{2,1,0:T(8,128)(2,1)}, u32[]{:S(2)}) copy-start(bf16[64,128,128]{2,1,0:T(8,128)(2,1)} %param.8) | copy-start | bytes 6291460
  0.0 3.1 %copy-start.5 = (bf16[128,128]{1,0:T(8,128)(2,1)S(1)}, bf16[128,128]{1,0:T(8,128)(2,1)}, u32[]{:S(2)}) copy-start(bf16[128,128]{1,0:T(8,128)(2,1)} %param.11) | copy-start | bytes 98308
  7.1 12.0 %copy-start.2 = (bf16[128,128]{1,0:T(8,128)(2,1)S(1)}, bf16[128,128]{1,0:T(8,128)(2,1)}, u32[]{:S(2)}) copy-start(bf16[128,128]{1,0:T(8,128)(2,1)} %param.10) | copy-start | bytes 98308
  7.1 40.7 %all-to-all-start = ((bf16[128,64,128]{2,1,0:T(8,128)(2,1)}), bf16[128,64,128]{2,1,0:T(8,128)(2,1)}, u32[]{:S(2)}, u32[]{:S(2)}) async-start(bf16[128,64,128]{2,1,0:T(8,128)(2,1)} %copy.24), calls=%async_computation | async-start | bytes 4194304 | tf_op jit(solution)/shard_map/all_to_all | solution.py:25
  19.1 0.8 copy-start.6
  47.8 34.8 %all-to-all-start.1 = ((bf16[128,64,128]{2,1,0:T(8,128)(2,1)}), bf16[128,64,128]{2,1,0:T(8,128)(2,1)}, u32[]{:S(2)}, u32[]{:S(2)}) async-start(bf16[128,64,128]{2,1,0:T(8,128)(2,1)} %copy.28), calls=%async_computation.1 | async-start | bytes 4194304 | tf_op jit(solution)/shard_map/all_to_all | solution.py:26
  82.6 3.5 %copy-start.1 = (bf16[16,8,64,128]{3,1,2,0:T(8,128)(2,1)S(1)}, bf16[16,8,64,128]{3,1,2,0:T(8,128)(2,1)}, u32[]{:S(2)}) copy-start(bf16[16,8,64,128]{3,1,2,0:T(8,128)(2,1)} %copy.25) | copy-start | bytes 6291460
  124.2 1.0 copy-start.4
  125.2 0.8 copy-start.3
  126.0 2.5 %copy-start.7 = (bf16[128,128]{1,0:T(8,128)(2,1)S(1)}, bf16[128,128]{1,0:T(8,128)(2,1)}, u32[]{:S(2)}) copy-start(bf16[128,128]{1,0:T(8,128)(2,1)} %param.15) | copy-start | bytes 98308

commit v2 on v1

v2 whole, which is shorter than its diff:
```python
import functools

import jax
import jax.numpy as jnp
from jax import lax
from jax.experimental import pallas as pl
from jax.experimental.pallas import tpu as pltpu
from jax.sharding import PartitionSpec as P

MESH = pl.DeviceIdType.MESH


def position():
    pr, pc = lax.axis_index("pr"), lax.axis_index("pc")
    return pc % 4, (pr // 2) % 4, (pc // 4) * 2 + pr // 8, pr % 2


def device(x, y, z, c):
    return ((z % 2) * 4 + y) * 2 + c, (z // 2) * 4 + x


def partner(here, code, parity):
    x, y, z, c = here
    dx, dy, dz, dc = 2 * (code % 2) + parity, (code // 2) % 4, (code // 8) % 4, code // 32
    return device((x + dx) % 4, (y + dy) % 4, (z + dz) % 4, (c + dc) % 2)


def exchange_kernel(
    scale, left_ref, right_ref, out_ref, lines, strips, sums, send_sem, recv_sem
):
    here = position()
    x = here[0]
    pr, pc = lax.axis_index("pr"), lax.axis_index("pc")
    mine = pr * 8 + pc
    slot = (pc // 4) * 2 + x // 2

    barrier = pltpu.get_barrier_semaphore()

    def greet(parity):
        def body(code, carry):
            pl.semaphore_signal(
                barrier, inc=1, device_id=partner(here, code, parity), device_id_type=MESH
            )
            return carry

        return body

    lax.fori_loop(1, 64, greet(0), 0)
    lax.fori_loop(0, 64, greet(1), 0)
    pl.semaphore_wait(barrier, 127)

    def send(source, target, index, to):
        pltpu.make_async_remote_copy(
            source, target, send_sem.at[index], recv_sem.at[index], device_id=to, device_id_type=MESH
        ).start()

    row, column = pl.multiple_of(pr * 64, 64), pl.multiple_of(pc * 128, 128)
    across = pl.multiple_of(slot * 128, 128)

    def send_left(parity):
        def body(step, carry):
            to = partner(here, (step * 37) % 64, parity)
            send(
                left_ref.at[to[0] * 8 + to[1]],
                lines.at[pl.ds(row, 64), pl.ds(column, 128)],
                0,
                to,
            )
            return carry

        return body

    def send_right(parity):
        def body(step, carry):
            to = partner(here, (step * 37) % 64, parity)
            send(
                right_ref.at[to[0] * 8 + to[1]],
                strips.at[parity, pl.ds(row, 64), pl.ds(across, 128)],
                1 + parity,
                to,
            )
            return carry

        return body

    def send_sums(parity):
        def body(step, carry):
            to = partner(here, (step * 37) % 64, parity)
            place = (to[1] // 4) * 2 + (to[1] % 4) // 2
            send(
                sums.at[parity, place, pl.ds(pl.multiple_of(to[0] * 64, 64), 64)],
                out_ref.at[mine],
                3 + parity,
                to,
            )
            return carry

        return body

    lax.fori_loop(1, 64, send_left(0), 0)
    lax.fori_loop(0, 64, send_left(1), 0)
    lax.fori_loop(1, 64, send_right(0), 0)
    lax.fori_loop(0, 64, send_right(1), 0)
    lines[pl.ds(row, 64), pl.ds(column, 128)] = left_ref[mine]
    strips[0, pl.ds(row, 64), pl.ds(across, 128)] = right_ref[mine]

    whole = (
        lines.at[pl.ds(0, 1016)],
        strips.at[0, pl.ds(0, 1008)],
        strips.at[1],
        sums.at[0, 0, pl.ds(0, 1008)],
        sums.at[0, 0],
    )
    parts = (1, 1, 1, 4, 4)

    def settle(sem, index):
        pltpu.make_async_copy(whole[index], whole[index], sem.at[index]).wait()

    settle(recv_sem, 0)
    for parity in (0, 1):
        settle(recv_sem, 1 + parity)

        def block(at, carry):
            start = pl.multiple_of(at * 128, 128)
            product = lax.dot_general(
                lines[:, pl.ds(start, 128)],
                strips[parity],
                (((0,), (0,)), ((), ())),
                preferred_element_type=jnp.float32,
            )
            product = (product * scale).astype(jnp.bfloat16)
            for place in range(4):
                sums[parity, place, pl.ds(start, 128)] = product[:, place * 128 : place * 128 + 128]
            return carry

        lax.fori_loop(0, 8, block, 0)
        if parity == 0:
            lax.fori_loop(1, 64, send_sums(0), 0)
        else:
            lax.fori_loop(0, 64, send_sums(1), 0)
    out_ref[mine] = sums[0, slot, pl.ds(row, 64)]

    for sem in (recv_sem, send_sem):
        pltpu.make_async_copy(out_ref.at[pl.ds(0, 63)], out_ref.at[pl.ds(0, 63)], sem.at[3]).wait()
        pltpu.make_async_copy(out_ref.at[pl.ds(0, 64)], out_ref.at[pl.ds(0, 64)], sem.at[4]).wait()
    for index in range(3):
        settle(send_sem, index)


def exchange(left, right):
    return pl.pallas_call(
        functools.partial(exchange_kernel, 1024 ** (-0.5)),
        out_shape=jax.ShapeDtypeStruct(left.shape, left.dtype),
        in_specs=[pl.BlockSpec(memory_space=pltpu.VMEM)] * 2,
        out_specs=pl.BlockSpec(memory_space=pltpu.VMEM),
        scratch_shapes=[
            pltpu.VMEM((1024, 1024), jnp.bfloat16),
            pltpu.VMEM((2, 1024, 512), jnp.bfloat16),
            pltpu.VMEM((2, 4, 1024, 128), jnp.bfloat16),
            pltpu.SemaphoreType.DMA((5,)),
            pltpu.SemaphoreType.DMA((5,)),
        ],
        compiler_params=pltpu.CompilerParams(
            collective_id=0, has_side_effects=True, vmem_limit_bytes=32 * 1024 * 1024
        ),
        name="exchange",
    )(left, right)


def factor(pair_in, weight, gate):
    value = jnp.einsum("ijc,cd->ijd", pair_in, weight, preferred_element_type=jnp.float32)
    value = value * jax.nn.sigmoid(
        jnp.einsum("ijc,cd->ijd", pair_in, gate, preferred_element_type=jnp.float32)
    )
    return jnp.moveaxis(value.astype(jnp.bfloat16), 2, 0)


def on_device(
    pair_array, left_weight, right_weight, left_gate, right_gate, mid_gain, out_weight, out_gate
):
    mixed = exchange(
        factor(pair_array, left_weight, left_gate), factor(pair_array, right_weight, right_gate)
    )
    values = mixed.astype(jnp.float32)
    centred = values - jnp.mean(values, axis=0, keepdims=True)
    scaled = (
        centred
        * lax.rsqrt(jnp.mean(centred * centred, axis=0, keepdims=True) + 1e-05)
        * mid_gain[:, None, None]
    ).astype(jnp.bfloat16)
    gate = jax.nn.sigmoid(
        jnp.einsum("ijc,cd->ijd", pair_array, out_gate, preferred_element_type=jnp.float32)
    )
    return (
        jnp.einsum("dij,dc->ijc", scaled, out_weight, preferred_element_type=jnp.float32) * gate
    ).astype(jnp.bfloat16)


def solution(mesh):
    return jax.shard_map(
        on_device,
        mesh=mesh,
        in_specs=(P("pr", "pc", None), P(), P(), P(), P(), P(), P(), P()),
        out_specs=P("pr", "pc", None),
        check_vma=False,
    )
```

time: 132 us -> 117 us (0.89)
  Pallas kernels: 0 us -> 86.8 us
  waiting for transfers between devices: 48 us -> 0 us
  blocking collectives: 34.5 us -> 0 us
  starting transfers between devices: 18 us -> 0 us
  other arithmetic: 1.68 us -> 19.2 us
  local copies, waits for them, and re-layouts: 16.4 us -> 1.65 us
  matrix products: 12.4 us -> 8.83 us
    pallas_call x0 -> x1, Pallas kernels: none -> 86.8 us  [exchange(): pl.pallas_call(functools.partial(exchange_kernel, 1024 ** (-0.5)), out_sh...]
    all_to_all x2 -> x0, waiting for transfers between devices: 48 us -> none  [the longest x1 24 us: on_device(): lax.all_to_all(jnp.moveaxis(right, 2, 0), BOTH, split_axis=0, concat_axis...]
    all_to_all x1 -> x0, blocking collectives: 34.5 us -> none  [on_device(): mixed = lax.all_to_all(mixed, BOTH, split_axis=0, concat_axis=0, tiled=True)]
    all_to_all x2 -> x0, starting transfers between devices: 18 us -> none  [the longest x1 11.9 us: on_device(): lax.all_to_all(jnp.moveaxis(left, 2, 0), BOTH, split_axis=0, concat_axis=...]
    convert_element_type x0 -> x1, other arithmetic: none -> 17.5 us  [factor(): return jnp.moveaxis(value.astype(jnp.bfloat16), 2, 0)]
    reshape x3 -> x0, local copies, waits for them, and re-layouts: 8.8 us -> none  [the longest x1 4.67 us: on_device(): left = left.reshape(pr, pc, rows, columns)]
    convert_element_type x2 -> x0, local copies, waits for them, and re-layouts: 5.34 us -> none  [factor(): return value.astype(jnp.bfloat16)]
    dot_general x1 -> x0, matrix products: 2.4 us -> none  [on_device(): jnp.einsum('ki,kj->ij', left, right, preferred_element_type=jnp.float32)]
  transfers between devices with their start and end apart: 2 -> 0, of which waited for: 2 -> 0; matrix products, arithmetic and copies ran while one was open for 7% -> 0% of each run, Pallas kernels for 0% -> 0%
where the time goes in v2:
time: 117 us
  Pallas kernels  86.8 us (74%)
  other arithmetic  19.2 us (16%)
  matrix products  8.83 us (8%)
  local copies, waits for them, and re-layouts  1.65 us (1%)
    pallas_call x1, Pallas kernels, exchange(): pl.pallas_call(functools.partial(exchange_kernel, 1024 ** (-0.5)), out_sh...  86.8 us
    convert_element_type x1, other arithmetic, factor(): return jnp.moveaxis(value.astype(jnp.bfloat16), 2, 0)  17.5 us
    dot_general x1, matrix products, on_device(): jnp.einsum('ijc,cd->ijd', pair_array, out_gate, preferred_element_type=jn...  2.64 us
    dot_general x1, matrix products, on_device(): jnp.einsum('dij,dc->ijc', scaled, out_weight, preferred_element_type=jnp....  2.51 us

profile of v2, /device:TPU:1, one launch (start us, length us, event | category | flops | bytes accessed | tf_op | source)
XLA Modules:
  0.0 116.6 jit_solution(14892961501250184868)
XLA Ops:
  0.0 0.0 copy-start
  0.0 0.0 copy-start.1
  0.0 1.6 %copy-done = bf16[64,128,128]{2,1,0:T(8,128)(2,1)S(1)} copy-done((bf16[64,128,128]{2,1,0:T(8,128)(2,1)S(1)}, bf16[64,128,128]{2,1,0:T(8,128)(2,1)}, u32[]{:S(2)}) %copy-start) | copy-done | bytes 2097176
  1.6 1.5 %fusion.23 = f32[128,64,128]{2,0,1:T(8,128)S(1)} fusion(bf16[64,128,128]{2,1,0:T(8,128)(2,1)S(1)} %copy-done, bf16[128,128]{1,0:T(8,128)(2,1)} %param.9), kind=kOutput, calls=%fused_computation.30 | convolution fusion | flops 268435456 | bytes 6324224 | tf_op jit(solution)/shard_map/ijc,cd->ijd/dot_general | solution.py:171
  3.1 0.0 copy-done.1
  3.1 0.0 copy-start.2
  3.1 0.7 fusion.19
  3.8 0.0 copy-done.2
  3.9 0.7 fusion.21
  4.6 0.0 copy-done.3
  4.6 0.7 fusion.17
  5.3 17.5 %fusion.5 = (bf16[128,64,128]{2,1,0:T(8,128)(2,1)S(1)}, bf16[128,64,128]{2,1,0:T(8,128)(2,1)S(1)}) fusion(f32[128,64,128]{2,0,1:T(8,128)S(1)} %fusion.19, f32[128,64,128]{2,0,1:T(8,128)S(1)} %fusion.17, f32[128,64,128]{2,0,1:T(8,128)S(1)} %fusion.21, f32[128,64,128]{2,0,1:T(8,128)S(1)} %fusion.23), kind=kLoop, calls=%fused_computation.8 | loop fusion | flops 10485760 | bytes 20971520 | tf_op jit(solution)/shard_map/convert_element_type | solution.py:175
  22.9 0.0 copy-start.5
  22.9 86.8 %exchange.1 = bf16[128,64,128]{2,1,0:T(8,128)(2,1)S(1)} custom-call(bf16[128,64,128]{2,1,0:T(8,128)(2,1)S(1)} %get-tuple-element.6.left_ref, bf16[128,64,128]{2,1,0:T(8,128)(2,1)S(1)} %get-tuple-element.5.right_ref), custom_call_target="tpu_custom_call" | custom-call | tf_op jit(solution)/shard_map/exchange/pallas_call | solution.py:151
  109.7 0.0 copy-start.4
  109.7 0.4 convert_reduce_fusion
  110.1 0.6 fusion.2
  110.7 0.0 copy-done.5
  110.7 0.7 fusion.4
  111.4 0.0 copy-done.4
  111.4 0.0 copy-start.6
  111.4 2.5 %fusion.13 = f32[64,128,128]{2,1,0:T(8,128)S(1)} fusion(bf16[128,64,128]{2,1,0:T(8,128)(2,1)S(1)} %fusion.4, bf16[128,128]{1,0:T(8,128)(2,1)S(1)} %copy-done.4), kind=kOutput, calls=%fused_computation.20 | convolution fusion | flops 268435456 | bytes 6324224 | tf_op jit(solution)/shard_map/dij,dc->ijc/dot_general | solution.py:195
  114.0 0.0 copy-done.6
  114.0 2.6 %multiply_convert_fusion = bf16[64,128,128]{2,1,0:T(8,128)(2,1)} fusion(f32[64,128,128]{2,1,0:T(8,128)S(1)} %fusion.13, bf16[64,128,128]{2,1,0:T(8,128)(2,1)S(1)} %copy-done, bf16[128,128]{1,0:T(8,128)(2,1)S(1)} %copy-done.6), kind=kOutput, calls=%fused_computation.19 | convolution fusion | flops 273678336 | bytes 8421376 | tf_op jit(solution)/shard_map/ijc,cd->ijd/dot_general | solution.py:192
  (3 shorter events, 0.0 us)
Async XLA Ops:
  0.0 1.6 %copy-start = (bf16[64,128,128]{2,1,0:T(8,128)(2,1)S(1)}, bf16[64,128,128]{2,1,0:T(8,128)(2,1)}, u32[]{:S(2)}) copy-start(bf16[64,128,128]{2,1,0:T(8,128)(2,1)} %param.8) | copy-start | bytes 6291460
  0.0 3.1 %copy-start.1 = (bf16[128,128]{1,0:T(8,128)(2,1)S(1)}, bf16[128,128]{1,0:T(8,128)(2,1)}, u32[]{:S(2)}) copy-start(bf16[128,128]{1,0:T(8,128)(2,1)} %param.10) | copy-start | bytes 98308
  3.1 0.8 copy-start.2
  3.9 0.8 copy-start.3
  22.9 87.8 %copy-start.5 = (f32[128]{0:T(128)S(1)}, f32[128]{0:T(128)}, u32[]{:S(2)}) copy-start(f32[128]{0:T(128)} %param.13) | copy-start | bytes 1540
  109.7 1.7 %copy-start.4 = (bf16[128,128]{1,0:T(8,128)(2,1)S(1)}, bf16[128,128]{1,0:T(8,128)(2,1)}, u32[]{:S(2)}) copy-start(bf16[128,128]{1,0:T(8,128)(2,1)} %param.14) | copy-start | bytes 98308
  111.4 2.5 %copy-start.6 = (bf16[128,128]{1,0:T(8,128)(2,1)S(1)}, bf16[128,128]{1,0:T(8,128)(2,1)}, u32[]{:S(2)}) copy-start(bf16[128,128]{1,0:T(8,128)(2,1)} %param.15) | copy-start | bytes 98308

commit v3 on v1

v3 whole, which is shorter than its diff:
```python
import functools

import jax
import jax.numpy as jnp
from jax import lax
from jax.experimental import pallas as pl
from jax.experimental.pallas import tpu as pltpu
from jax.sharding import PartitionSpec as P

MESH = pl.DeviceIdType.MESH


def position():
    pr, pc = lax.axis_index("pr"), lax.axis_index("pc")
    return pc % 4, (pr // 2) % 4, (pc // 4) * 2 + pr // 8, pr % 2


def device(x, y, z, c):
    return ((z % 2) * 4 + y) * 2 + c, (z // 2) * 4 + x


def partner(here, code, parity):
    x, y, z, c = here
    dx, dy, dz, dc = 2 * (code % 2) + parity, (code // 2) % 4, (code // 8) % 4, code // 32
    return device((x + dx) % 4, (y + dy) % 4, (z + dz) % 4, (c + dc) % 2)


def triangle_kernel(
    scale,
    pair_hbm,
    left_weight,
    right_weight,
    left_gate,
    right_gate,
    gain_ref,
    out_weight,
    out_gate,
    out_ref,
    pair,
    turned,
    gains,
    stage,
    left_send,
    right_send,
    lines,
    strips,
    sums,
    mixed,
    gate,
    load_sem,
    send_sem,
    recv_sem,
):
    here = position()
    x = here[0]
    pr, pc = lax.axis_index("pr"), lax.axis_index("pc")
    mine = pr * 8 + pc
    slot = (pc // 4) * 2 + x // 2
    row, column = pl.multiple_of(pr * 64, 64), pl.multiple_of(pc * 128, 128)
    across = pl.multiple_of(slot * 128, 128)

    load = pltpu.make_async_copy(pair_hbm, pair, load_sem)
    load.start()
    barrier = pltpu.get_barrier_semaphore()

    def partners(visit):
        def even(step, carry):
            visit(0, partner(here, (step * 37) % 64, 0))
            return carry

        def odd(step, carry):
            visit(1, partner(here, (step * 37) % 64, 1))
            return carry

        return lambda: lax.fori_loop(1, 64, even, 0), lambda: lax.fori_loop(0, 64, odd, 0)

    def greet(parity, to):
        pl.semaphore_signal(barrier, inc=1, device_id=to, device_id_type=MESH)

    for run in partners(greet):
        run()

    def send(source, target, index, to):
        pltpu.make_async_remote_copy(
            source, target, send_sem.at[index], recv_sem.at[index], device_id=to, device_id_type=MESH
        ).start()

    for index, ref in enumerate((left_weight, left_gate, right_weight, right_gate)):
        turned[index] = ref[...].astype(jnp.float32).T.astype(jnp.bfloat16)
    gains[...] = jnp.broadcast_to(gain_ref[...], (128, 128)).T

    def factor(index, first, target):
        for pair_at in range(8):
            both = pair[pl.ds(first + 2 * pair_at, 2)].reshape(256, 128)
            value = lax.dot_general(
                turned[index], both, (((1,), (1,)), ((), ())), preferred_element_type=jnp.float32
            )
            level = lax.dot_general(
                turned[index + 1], both, (((1,), (1,)), ((), ())), preferred_element_type=jnp.float32
            )
            value = value * jax.nn.sigmoid(level)
            stage[2 * pair_at] = value[:, :128]
            stage[2 * pair_at + 1] = value[:, 128:]

        def turn(at, carry):
            channel = pl.multiple_of(at * 8, 8)
            target[pl.ds(channel, 8)] = jnp.swapaxes(stage[:16, pl.ds(channel, 8), :], 0, 1).astype(
                jnp.bfloat16
            )
            return carry

        lax.fori_loop(0, 16, turn, 0)

    load.wait()
    for half in range(2):

        def left_rows(at, carry):
            start = pl.multiple_of(at * 16, 16)
            factor(0, half * 32 + start, left_send.at[half, :, pl.ds(start, 16)])
            return carry

        lax.fori_loop(0, 2, left_rows, 0)
        if half == 0:
            pl.semaphore_wait(barrier, 127)

        def send_left(parity, to):
            send(
                left_send.at[half, to[0] * 8 + to[1]],
                lines.at[pl.ds(pl.multiple_of(row + half * 32, 32), 32), pl.ds(column, 128)],
                half,
                to,
            )

        for run in partners(send_left):
            run()

    def right_rows(at, carry):
        start = pl.multiple_of(at * 16, 16)
        factor(2, start, right_send.at[:, pl.ds(start, 16)])
        return carry

    lax.fori_loop(0, 4, right_rows, 0)

    def send_right(parity, to):
        send(
            right_send.at[to[0] * 8 + to[1]],
            strips.at[parity, pl.ds(row, 64), pl.ds(across, 128)],
            2 + parity,
            to,
        )

    for run in partners(send_right):
        run()

    lines[pl.ds(row, 32), pl.ds(column, 128)] = left_send[0, mine]
    lines[pl.ds(pl.multiple_of(row + 32, 32), 32), pl.ds(column, 128)] = left_send[1, mine]
    strips[0, pl.ds(row, 64), pl.ds(across, 128)] = right_send[mine]

    def gate_rows(at, carry):
        start = at * 4
        level = jnp.dot(
            pair[pl.ds(start, 4)].reshape(512, 128),
            out_gate[...],
            preferred_element_type=jnp.float32,
        )
        gate[pl.ds(start, 4)] = jax.nn.sigmoid(level).reshape(4, 128, 128)
        return carry

    lax.fori_loop(0, 16, gate_rows, 0)

    def settle(ref, sem):
        pltpu.make_async_copy(ref, ref, sem).wait()

    settle(left_send.at[0, pl.ds(0, 127)], recv_sem.at[0])
    settle(left_send.at[1, pl.ds(0, 127)], recv_sem.at[1])
    for parity in (0, 1):
        settle(strips.at[parity, pl.ds(0, 1008 + 16 * parity)], recv_sem.at[2 + parity])

        def block(at, carry):
            start = pl.multiple_of(at * 128, 128)
            product = lax.dot_general(
                lines[:, pl.ds(start, 128)],
                strips[parity],
                (((0,), (0,)), ((), ())),
                preferred_element_type=jnp.float32,
            )
            product = (product * scale).astype(jnp.bfloat16)
            for place in range(4):
                sums[parity, place, pl.ds(start, 128)] = product[:, place * 128 : place * 128 + 128]
            return carry

        lax.fori_loop(0, 8, block, 0)

        for first, size, index in ((0, 64, 4),) if parity == 0 else ((0, 32, 5), (32, 32, 6)):

            def send_sums(_, to):
                place = (to[1] // 4) * 2 + (to[1] % 4) // 2
                send(
                    sums.at[parity, place, pl.ds(pl.multiple_of(to[0] * 64 + first, size), size)],
                    mixed.at[mine, pl.ds(first, size)],
                    index,
                    to,
                )

            partners(send_sums)[parity]()
    mixed[mine] = sums[0, slot, pl.ds(row, 64)]

    def finish(at, carry):
        start = pl.multiple_of(at * 16, 16)

        def turn(group, carry):
            channel = pl.multiple_of(group * 8, 8)
            stage[:, pl.ds(channel, 8), :] = jnp.swapaxes(
                mixed[pl.ds(channel, 8), pl.ds(start, 16), :].astype(jnp.float32), 0, 1
            )
            return carry

        lax.fori_loop(0, 16, turn, 0)

        def line(inner, carry):
            values = stage[inner]
            centred = values - jnp.mean(values, axis=0, keepdims=True)
            spread = lax.rsqrt(jnp.mean(centred * centred, axis=0, keepdims=True) + 1e-05)
            scaled = (centred * spread * gains[...]).astype(jnp.bfloat16)
            product = lax.dot_general(
                scaled,
                out_weight[...],
                (((0,), (0,)), ((), ())),
                preferred_element_type=jnp.float32,
            )
            out_ref[start + inner] = (product * gate[start + inner]).astype(jnp.bfloat16)
            return carry

        lax.fori_loop(0, 16, line, 0, unroll=4)
        return carry

    settle(mixed.at[pl.ds(0, 63)], recv_sem.at[4])
    settle(mixed.at[pl.ds(0, 32)], recv_sem.at[5])
    lax.fori_loop(0, 2, finish, 0)
    settle(mixed.at[pl.ds(0, 32)], recv_sem.at[6])
    lax.fori_loop(2, 4, finish, 0)

    settle(left_send.at[0, pl.ds(0, 127)], send_sem.at[0])
    settle(left_send.at[1, pl.ds(0, 127)], send_sem.at[1])
    settle(strips.at[0, pl.ds(0, 1008)], send_sem.at[2])
    settle(strips.at[1], send_sem.at[3])
    settle(mixed.at[pl.ds(0, 63)], send_sem.at[4])
    settle(mixed.at[pl.ds(0, 32)], send_sem.at[5])
    settle(mixed.at[pl.ds(0, 32)], send_sem.at[6])


def on_device(
    pair_array, left_weight, right_weight, left_gate, right_gate, mid_gain, out_weight, out_gate
):
    half, single = jnp.bfloat16, jnp.float32
    return pl.pallas_call(
        functools.partial(triangle_kernel, 1024 ** (-0.5)),
        out_shape=jax.ShapeDtypeStruct(pair_array.shape, half),
        in_specs=[pl.BlockSpec(memory_space=pl.ANY)] + [pl.BlockSpec(memory_space=pltpu.VMEM)] * 7,
        out_specs=pl.BlockSpec(memory_space=pltpu.VMEM),
        scratch_shapes=[
            pltpu.VMEM((64, 128, 128), half),
            pltpu.VMEM((4, 128, 128), half),
            pltpu.VMEM((128, 128), single),
            pltpu.VMEM((16, 128, 128), single),
            pltpu.VMEM((2, 128, 32, 128), half),
            pltpu.VMEM((128, 64, 128), half),
            pltpu.VMEM((1024, 1024), half),
            pltpu.VMEM((2, 1024, 512), half),
            pltpu.VMEM((2, 4, 1024, 128), half),
            pltpu.VMEM((128, 64, 128), half),
            pltpu.VMEM((64, 128, 128), single),
            pltpu.SemaphoreType.DMA,
            pltpu.SemaphoreType.DMA((7,)),
            pltpu.SemaphoreType.DMA((7,)),
        ],
        compiler_params=pltpu.CompilerParams(
            collective_id=0, has_side_effects=True, vmem_limit_bytes=48 * 1024 * 1024
        ),
        name="triangle",
    )(
        pair_array,
        left_weight,
        right_weight,
        left_gate,
        right_gate,
        mid_gain.reshape(1, 128),
        out_weight,
        out_gate,
    )


def solution(mesh):
    return jax.shard_map(
        on_device,
        mesh=mesh,
        in_specs=(P("pr", "pc", None), P(), P(), P(), P(), P(), P(), P()),
        out_specs=P("pr", "pc", None),
        check_vma=False,
    )
```

time: 132 us -> 104 us (0.79)
  Pallas kernels: 0 us -> 95.5 us
  waiting for transfers between devices: 48 us -> 0 us
  blocking collectives: 34.5 us -> 0 us
  starting transfers between devices: 18 us -> 0 us
  matrix products: 12.4 us -> 0 us
  local copies, waits for them, and re-layouts: 16.4 us -> 8.11 us
  other arithmetic: 1.68 us -> 0 us
    pallas_call x0 -> x1, Pallas kernels: none -> 95.5 us  [on_device(): pl.pallas_call(functools.partial(triangle_kernel, 1024 ** (-0.5)), out_sh...]
    all_to_all x2 -> x0, waiting for transfers between devices: 48 us -> none  [the longest x1 24 us: on_device(): lax.all_to_all(jnp.moveaxis(right, 2, 0), BOTH, split_axis=0, concat_axis...]
    all_to_all x1 -> x0, blocking collectives: 34.5 us -> none  [on_device(): mixed = lax.all_to_all(mixed, BOTH, split_axis=0, concat_axis=0, tiled=True)]
    all_to_all x2 -> x0, starting transfers between devices: 18 us -> none  [the longest x1 11.9 us: on_device(): lax.all_to_all(jnp.moveaxis(left, 2, 0), BOTH, split_axis=0, concat_axis=...]
    dot_general x7 -> x0, matrix products: 12.4 us -> none  [the longest x2 2.67 us: factor(): jnp.einsum('ijc,cd->ijd', pair_in, gate, preferred_element_type=jnp.float32)]
    reshape x3 -> x0, local copies, waits for them, and re-layouts: 8.8 us -> none  [the longest x1 4.67 us: on_device(): left = left.reshape(pr, pc, rows, columns)]
    unnamed x17, local copies, waits for them, and re-layouts: 2.29 us -> 8.11 us
    convert_element_type x2 -> x0, local copies, waits for them, and re-layouts: 5.34 us -> none  [factor(): return value.astype(jnp.bfloat16)]
  transfers between devices with their start and end apart: 2 -> 0, of which waited for: 2 -> 0; matrix products, arithmetic and copies ran while one was open for 7% -> 0% of each run, Pallas kernels for 0% -> 0%
where the time goes in v3:
time: 104 us
  Pallas kernels  95.5 us (92%)
  local copies, waits for them, and re-layouts  8.11 us (8%)
    pallas_call x1, Pallas kernels, on_device(): pl.pallas_call(functools.partial(triangle_kernel, 1024 ** (-0.5)), out_sh...  95.5 us
    unnamed x17, local copies, waits for them, and re-layouts  8.11 us

profile of v3, /device:TPU:1, one launch (start us, length us, event | category | flops | bytes accessed | tf_op | source)
XLA Modules:
  0.0 103.6 jit_solution(17171482826850893161)
XLA Ops:
  0.0 0.0 copy-start
  0.0 1.6 %copy-done = bf16[64,128,128]{2,1,0:T(8,128)(2,1)S(1)} copy-done((bf16[64,128,128]{2,1,0:T(8,128)(2,1)S(1)}, bf16[64,128,128]{2,1,0:T(8,128)(2,1)}, u32[]{:S(2)}) %copy-start) | copy-done | bytes 2097176
  1.6 0.0 copy-start.1
  1.6 0.8 copy-done.1
  2.4 0.0 copy-start.2
  2.4 0.8 copy-done.2
  3.1 0.0 copy-start.3
  3.1 0.8 copy-done.3
  3.9 0.0 copy-start.4
  3.9 0.8 copy-done.4
  4.6 0.0 copy-start.5
  4.6 0.8 copy-done.5
  5.4 0.0 copy-start.6
  5.4 0.8 copy-done.6
  6.1 0.0 copy-start.7
  6.1 0.7 copy-done.7
  6.8 95.5 %triangle.1 = bf16[64,128,128]{2,1,0:T(8,128)(2,1)S(1)} custom-call(bf16[64,128,128]{2,1,0:T(8,128)(2,1)S(1)} %copy-done, bf16[128,128]{1,0:T(8,128)(2,1)S(1)} %copy-done.1, bf16[128,128]{1,0:T(8,128)(2,1)S(1)} %copy-done.2, bf16[128,128]{1,0:T(8,128)(2,1)S(1)} %copy-done.3, bf16[128,128]{1,0:T(8,128)(2,1)S(1)} %copy-done.4, f32[1,128]{1,0:T(1,128)S(1)} %bitcast.1, ...), custom_call_target="tpu_custom_call" | custom-call | tf_op jit(solution)/shard_map/triangle/pallas_call | solution.py:256
  102.3 1.3 %copy.10 = bf16[64,128,128]{2,1,0:T(8,128)(2,1)} copy(bf16[64,128,128]{2,1,0:T(8,128)(2,1)S(1)} %triangle.1) | data formatting | bytes 4194304
Async XLA Ops:
  0.0 1.6 %copy-start = (bf16[64,128,128]{2,1,0:T(8,128)(2,1)S(1)}, bf16[64,128,128]{2,1,0:T(8,128)(2,1)}, u32[]{:S(2)}) copy-start(bf16[64,128,128]{2,1,0:T(8,128)(2,1)} %pair_hbm.1) | copy-start | bytes 6291460
  1.6 0.8 copy-start.1
  2.4 0.8 copy-start.2
  3.1 0.8 copy-start.3
  3.9 0.8 copy-start.4
  4.6 0.8 copy-start.5
  5.4 0.8 copy-start.6
  6.1 0.7 copy-start.7

commit v4 on v3

v4 whole, which is shorter than its diff:
```python
import functools

import jax
import jax.numpy as jnp
from jax import lax
from jax.experimental import pallas as pl
from jax.experimental.pallas import tpu as pltpu
from jax.sharding import PartitionSpec as P

MESH = pl.DeviceIdType.MESH


def offsets():
    def negated(o):
        return tuple(-v % 4 for v in o)

    seen, sets = set(), []
    for code in range(64):
        o = (code // 16, code // 4 % 4, code % 4)
        if o in seen:
            continue
        one = []
        for _ in range(3):
            for p in (o, negated(o)):
                if p not in one:
                    one.append(p)
            o = (o[2], o[0], o[1])
        seen.update(one)
        sets.append(one)
    sets.sort(key=lambda one: -sum(min(v, 4 - v) for v in one[0]))
    flat = [o for one in sets for o in one]
    order = [(*o, (at + turn) % 2) for turn in (0, 1) for at, o in enumerate(flat)]
    return [o for o in order if o != (0, 0, 0, 0)]


ORDER = offsets()
SIDES = [[o for o in ORDER if o[0] % 2 == parity] for parity in (0, 1)]


def triangle_kernel(
    scale,
    pair_hbm,
    left_weight_hbm,
    right_weight_hbm,
    left_gate_hbm,
    right_gate_hbm,
    gain_hbm,
    out_weight_hbm,
    out_gate_hbm,
    out_ref,
    pair,
    weights,
    gain_row,
    turned,
    gains,
    stage,
    left_send,
    right_send,
    lines,
    strips,
    sums,
    mixed,
    gate,
    load_sem,
    send_sem,
    recv_sem,
):
    pr, pc = lax.axis_index("pr"), lax.axis_index("pc")
    x, y, c = lax.rem(pc, 4), lax.rem(lax.div(pr, 2), 4), lax.rem(pr, 2)
    z = lax.div(pc, 4) * 2 + lax.div(pr, 8)
    mine = pr * 8 + pc
    slot = lax.div(pc, 4) * 2 + lax.div(x, 2)
    xs = [lax.rem(x + d, 4) for d in range(4)]
    ys = [lax.rem(y + d, 4) * 2 for d in range(4)]
    zs = [lax.rem(z + d, 4) for d in range(4)]
    rows_of = [[lax.rem(v, 2) * 8 + w for w in ys] for v in zs]
    columns_of = [[lax.div(v, 2) * 4 + w for w in xs] for v in zs]
    places_of = [[lax.div(v, 2) * 2 + lax.div(w, 2) for w in xs] for v in zs]
    cores = [c, 1 - c]

    def partner(o):
        dx, dy, dz, dc = o
        return rows_of[dz][dy] + cores[dc], columns_of[dz][dx]

    row, column = pl.multiple_of(pr * 64, 64), pl.multiple_of(pc * 128, 128)
    across = pl.multiple_of(slot * 128, 128)

    matrices = (
        left_weight_hbm,
        left_gate_hbm,
        right_weight_hbm,
        right_gate_hbm,
        out_weight_hbm,
        out_gate_hbm,
    )
    loads = [
        pltpu.make_async_copy(ref, weights.at[index], load_sem.at[index])
        for index, ref in enumerate(matrices)
    ]
    loads.append(pltpu.make_async_copy(gain_hbm, gain_row, load_sem.at[6]))
    pair_loads = [
        pltpu.make_async_copy(
            pair_hbm.at[pl.ds(first, 32)], pair.at[pl.ds(first, 32)], load_sem.at[7 + first // 32]
        )
        for first in (0, 32)
    ]
    for load in loads + pair_loads:
        load.start()
    barrier = pltpu.get_barrier_semaphore()

    with jax.named_scope("greet"):
        for o in ORDER:
            pl.semaphore_signal(barrier, inc=1, device_id=partner(o), device_id_type=MESH)

    def send(source, target, index, to):
        pltpu.make_async_remote_copy(
            source, target, send_sem.at[index], recv_sem.at[index], device_id=to, device_id_type=MESH
        ).start()

    with jax.named_scope("weights"):
        for load in loads:
            load.wait()
        for index in range(4):
            turned[index] = weights[index].astype(jnp.float32).T.astype(jnp.bfloat16)
        gains[...] = jnp.broadcast_to(gain_row[...], (128, 128)).T

    def factor(index, first, target):
        for pair_at in range(8):
            both = pair[pl.ds(first + 2 * pair_at, 2)].reshape(256, 128)
            value = lax.dot_general(
                turned[index], both, (((1,), (1,)), ((), ())), preferred_element_type=jnp.float32
            )
            level = lax.dot_general(
                turned[index + 1], both, (((1,), (1,)), ((), ())), preferred_element_type=jnp.float32
            )
            value = value * jax.nn.sigmoid(level)
            stage[2 * pair_at] = value[:, :128]
            stage[2 * pair_at + 1] = value[:, 128:]

        def turn(at, carry):
            channel = pl.multiple_of(at * 8, 8)
            target[pl.ds(channel, 8)] = jnp.swapaxes(stage[:16, pl.ds(channel, 8), :], 0, 1).astype(
                jnp.bfloat16
            )
            return carry

        lax.fori_loop(0, 16, turn, 0)

    for half in range(2):
        with jax.named_scope("wait_pair"):
            pair_loads[half].wait()

        def left_rows(at, carry):
            start = pl.multiple_of(at * 16, 16)
            factor(0, half * 32 + start, left_send.at[half, :, pl.ds(start, 16)])
            return carry

        with jax.named_scope("left_rows"):
            lax.fori_loop(0, 2, left_rows, 0)
        if half == 0:
            with jax.named_scope("wait_barrier"):
                pl.semaphore_wait(barrier, 127)

        with jax.named_scope("send_left"):
            for o in ORDER:
                to = partner(o)
                send(
                    left_send.at[half, to[0] * 8 + to[1]],
                    lines.at[pl.ds(pl.multiple_of(row + half * 32, 32), 32), pl.ds(column, 128)],
                    half,
                    to,
                )

    def right_rows(at, carry):
        start = pl.multiple_of(at * 16, 16)
        factor(2, start, right_send.at[:, pl.ds(start, 16)])
        return carry

    with jax.named_scope("right_rows"):
        lax.fori_loop(0, 4, right_rows, 0)

    with jax.named_scope("send_right"):
        for parity in (0, 1):
            for o in SIDES[parity]:
                to = partner(o)
                send(
                    right_send.at[to[0] * 8 + to[1]],
                    strips.at[parity, pl.ds(row, 64), pl.ds(across, 128)],
                    2 + parity,
                    to,
                )

    lines[pl.ds(row, 32), pl.ds(column, 128)] = left_send[0, mine]
    lines[pl.ds(pl.multiple_of(row + 32, 32), 32), pl.ds(column, 128)] = left_send[1, mine]
    strips[0, pl.ds(row, 64), pl.ds(across, 128)] = right_send[mine]

    def gate_rows(at, carry):
        start = at * 4
        level = jnp.dot(
            pair[pl.ds(start, 4)].reshape(512, 128),
            weights[5],
            preferred_element_type=jnp.float32,
        )
        gate[pl.ds(start, 4)] = jax.nn.sigmoid(level).reshape(4, 128, 128)
        return carry

    with jax.named_scope("gate"):
        lax.fori_loop(0, 16, gate_rows, 0)

    def settle(ref, sem):
        pltpu.make_async_copy(ref, ref, sem).wait()

    with jax.named_scope("wait_left"):
        settle(left_send.at[0, pl.ds(0, 127)], recv_sem.at[0])
        settle(left_send.at[1, pl.ds(0, 127)], recv_sem.at[1])
    for parity in (0, 1):
        with jax.named_scope("wait_right"):
            settle(strips.at[parity, pl.ds(0, 1008 + 16 * parity)], recv_sem.at[2 + parity])

        def block(at, carry):
            start = pl.multiple_of(at * 128, 128)
            product = lax.dot_general(
                lines[:, pl.ds(start, 128)],
                strips[parity],
                (((0,), (0,)), ((), ())),
                preferred_element_type=jnp.float32,
            )
            product = (product * scale).astype(jnp.bfloat16)
            for place in range(4):
                sums[parity, place, pl.ds(start, 128)] = product[:, place * 128 : place * 128 + 128]
            return carry

        with jax.named_scope("matmul"):
            lax.fori_loop(0, 8, block, 0)

        with jax.named_scope("send_sums"):
            for first, size, index in ((0, 64, 4),) if parity == 0 else ((0, 48, 5), (48, 16, 6)):
                for o in SIDES[parity]:
                    to = partner(o)
                    start = pl.multiple_of(to[0] * 64 + first, 16)
                    send(
                        sums.at[parity, places_of[o[2]][o[0]], pl.ds(start, size)],
                        mixed.at[mine, pl.ds(first, size)],
                        index,
                        to,
                    )
    mixed[mine] = sums[0, slot, pl.ds(row, 64)]

    def finish(at, carry):
        start = at * 16 if isinstance(at, int) else pl.multiple_of(at * 16, 16)

        def turn(group, carry):
            channel = pl.multiple_of(group * 8, 8)
            stage[:, pl.ds(channel, 8), :] = jnp.swapaxes(
                mixed[pl.ds(channel, 8), pl.ds(start, 16), :].astype(jnp.float32), 0, 1
            )
            return carry

        with jax.named_scope("turn"):
            lax.fori_loop(0, 16, turn, 0)

        def line(inner, carry):
            values = stage[inner]
            centred = values - jnp.mean(values, axis=0, keepdims=True)
            spread = lax.rsqrt(jnp.mean(centred * centred, axis=0, keepdims=True) + 1e-05)
            scaled = (centred * spread * gains[...]).astype(jnp.bfloat16)
            product = lax.dot_general(
                scaled,
                weights[4],
                (((0,), (0,)), ((), ())),
                preferred_element_type=jnp.float32,
            )
            out_ref[start + inner] = (product * gate[start + inner]).astype(jnp.bfloat16)
            return carry

        with jax.named_scope("line"):
            lax.fori_loop(0, 16, line, 0, unroll=4)
        return carry

    with jax.named_scope("wait_sums"):
        settle(mixed.at[pl.ds(0, 63)], recv_sem.at[4])
        settle(mixed.at[pl.ds(0, 48)], recv_sem.at[5])
    with jax.named_scope("finish_a"):
        lax.fori_loop(0, 3, finish, 0)
    with jax.named_scope("wait_last"):
        settle(mixed.at[pl.ds(0, 16)], recv_sem.at[6])
    with jax.named_scope("finish_b"):
        finish(3, 0)

    with jax.named_scope("drain"):
        settle(left_send.at[0, pl.ds(0, 127)], send_sem.at[0])
        settle(left_send.at[1, pl.ds(0, 127)], send_sem.at[1])
        settle(strips.at[0, pl.ds(0, 1008)], send_sem.at[2])
        settle(strips.at[1], send_sem.at[3])
        settle(mixed.at[pl.ds(0, 63)], send_sem.at[4])
        settle(mixed.at[pl.ds(0, 48)], send_sem.at[5])
        settle(mixed.at[pl.ds(0, 16)], send_sem.at[6])


def on_device(
    pair_array, left_weight, right_weight, left_gate, right_gate, mid_gain, out_weight, out_gate
):
    half, single = jnp.bfloat16, jnp.float32
    call = pl.pallas_call(
        functools.partial(triangle_kernel, 1024 ** (-0.5)),
        out_shape=jax.ShapeDtypeStruct(pair_array.shape, half),
        in_specs=[pl.BlockSpec(memory_space=pltpu.HBM)] * 8,
        out_specs=pl.BlockSpec(memory_space=pltpu.VMEM),
        scratch_shapes=[
            pltpu.VMEM((64, 128, 128), half),
            pltpu.VMEM((6, 128, 128), half),
            pltpu.VMEM((1, 128), single),
            pltpu.VMEM((4, 128, 128), half),
            pltpu.VMEM((128, 128), single),
            pltpu.VMEM((16, 128, 128), single),
            pltpu.VMEM((2, 128, 32, 128), half),
            pltpu.VMEM((128, 64, 128), half),
            pltpu.VMEM((1024, 1024), half),
            pltpu.VMEM((2, 1024, 512), half),
            pltpu.VMEM((2, 4, 1024, 128), half),
            pltpu.VMEM((128, 64, 128), half),
            pltpu.VMEM((64, 128, 128), single),
            pltpu.SemaphoreType.DMA((9,)),
            pltpu.SemaphoreType.DMA((7,)),
            pltpu.SemaphoreType.DMA((7,)),
        ],
        compiler_params=pltpu.CompilerParams(
            collective_id=0, has_side_effects=True, vmem_limit_bytes=50 * 1024 * 1024
        ),
        name="triangle",
    )
    operands = (
        pair_array,
        left_weight,
        right_weight,
        left_gate,
        right_gate,
        mid_gain.reshape(1, 128),
        out_weight,
        out_gate,
    )
    return call(*(pltpu.with_memory_space_constraint(a, pltpu.HBM) for a in operands))


def solution(mesh):
    return jax.shard_map(
        on_device,
        mesh=mesh,
        in_specs=(P("pr", "pc", None), P(), P(), P(), P(), P(), P(), P()),
        out_specs=P("pr", "pc", None),
        check_vma=False,
    )
```

time: 104 us -> 86.3 us (0.83)
  Pallas kernels: 95.5 us -> 84.5 us
  local copies, waits for them, and re-layouts: 8.11 us -> 1.32 us
    pallas_call x1, Pallas kernels: 95.5 us -> 84.5 us  [on_device(): call(*(pltpu.with_memory_space_constraint(a, pltpu.HBM) for a in operands))]
    unnamed x17 -> x1, local copies, waits for them, and re-layouts: 8.11 us -> 1.32 us
where the time goes in v4:
time: 86.3 us; the launch traced here: 85.8 us
  Pallas kernels  84.5 us (98%)
  local copies, waits for them, and re-layouts  1.32 us (2%)
    pallas_call x1, Pallas kernels, on_device(): call(*(pltpu.with_memory_space_constraint(a, pltpu.HBM) for a in operands))  84.5 us

profile of v4, /device:TPU:1, one launch (start us, length us, event | category | flops | bytes accessed | tf_op | source)
XLA Modules:
  0.0 85.8 jit_solution(10220163688241537825)
XLA Ops:
  0.0 84.5 %triangle.1 = bf16[64,128,128]{2,1,0:T(8,128)(2,1)S(1)} custom-call(bf16[64,128,128]{2,1,0:T(8,128)(2,1)} %pair_hbm.1, bf16[128,128]{1,0:T(8,128)(2,1)} %left_weight_hbm.1, bf16[128,128]{1,0:T(8,128)(2,1)} %right_weight_hbm.1, bf16[128,128]{1,0:T(8,128)(2,1)} %left_gate_hbm.1, bf16[128,128]{1,0:T(8,128)(2,1)} %right_gate_hbm.1, f32[1,128]{1,0:T(1,128)} %bitcast.1, ...), custom_call_target="tpu_custom_call" | custom-call | tf_op jit(solution)/shard_map/triangle/pallas_call | solution.py:342
  84.5 1.3 %copy.10 = bf16[64,128,128]{2,1,0:T(8,128)(2,1)} copy(bf16[64,128,128]{2,1,0:T(8,128)(2,1)S(1)} %triangle.1) | data formatting | bytes 4194304

commit v5 on v4

--- a/solution.py
+++ b/solution.py
@@ -34,6 +34,7 @@
 
 
 ORDER = offsets()
+PIECES = (((0, 4, 4),), ((0, 2, 5), (2, 1, 6), (3, 1, 7)))
 SIDES = [[o for o in ORDER if o[0] % 2 == parity] for parity in (0, 1)]
 
 
@@ -57,6 +58,7 @@
     left_send,
     right_send,
     lines,
+    lines_t,
     strips,
     sums,
     mixed,
@@ -70,9 +72,9 @@
     z = lax.div(pc, 4) * 2 + lax.div(pr, 8)
     mine = pr * 8 + pc
     slot = lax.div(pc, 4) * 2 + lax.div(x, 2)
-    xs = [lax.rem(x + d, 4) for d in range(4)]
-    ys = [lax.rem(y + d, 4) * 2 for d in range(4)]
-    zs = [lax.rem(z + d, 4) for d in range(4)]
+    xs = [lax.rem(x + d + c * (-2 * d % 4), 4) for d in range(4)]
+    ys = [lax.rem(y + d + c * (-2 * d % 4), 4) * 2 for d in range(4)]
+    zs = [lax.rem(z + d + c * (-2 * d % 4), 4) for d in range(4)]
     rows_of = [[lax.rem(v, 2) * 8 + w for w in ys] for v in zs]
     columns_of = [[lax.div(v, 2) * 4 + w for w in xs] for v in zs]
     places_of = [[lax.div(v, 2) * 2 + lax.div(w, 2) for w in xs] for v in zs]
@@ -213,38 +215,47 @@
     with jax.named_scope("wait_left"):
         settle(left_send.at[0, pl.ds(0, 127)], recv_sem.at[0])
         settle(left_send.at[1, pl.ds(0, 127)], recv_sem.at[1])
+    def turn_lines(at, carry):
+        block = lines[:, pl.ds(pl.multiple_of(at * 128, 128), 128)].T.reshape(2, 4, 16, 1024)
+        for quarter in range(4):
+            lines_t[quarter, pl.ds(at * 2, 2)] = block[:, quarter]
+        return carry
+
+    with jax.named_scope("turn_lines"):
+        lax.fori_loop(0, 8, turn_lines, 0)
+
     for parity in (0, 1):
         with jax.named_scope("wait_right"):
             settle(strips.at[parity, pl.ds(0, 1008 + 16 * parity)], recv_sem.at[2 + parity])
 
         def block(at, carry):
-            start = pl.multiple_of(at * 128, 128)
-            product = lax.dot_general(
-                lines[:, pl.ds(start, 128)],
+            quarter, group = lax.div(at, 2), lax.rem(at, 2) * 8
+            product = jnp.dot(
+                lines_t[quarter, pl.ds(group, 8)].reshape(128, 1024),
                 strips[parity],
-                (((0,), (0,)), ((), ())),
                 preferred_element_type=jnp.float32,
             )
             product = (product * scale).astype(jnp.bfloat16)
             for place in range(4):
-                sums[parity, place, pl.ds(start, 128)] = product[:, place * 128 : place * 128 + 128]
-            return carry
-
-        with jax.named_scope("matmul"):
-            lax.fori_loop(0, 8, block, 0)
-
-        with jax.named_scope("send_sums"):
-            for first, size, index in ((0, 64, 4),) if parity == 0 else ((0, 48, 5), (48, 16, 6)):
+                sums[parity, quarter, place, pl.ds(group, 8)] = product[
+                    :, place * 128 : place * 128 + 128
+                ].reshape(8, 16, 128)
+            return carry
+
+        for first, size, index in PIECES[parity]:
+            with jax.named_scope("matmul"):
+                lax.fori_loop(2 * first, 2 * (first + size), block, 0)
+            with jax.named_scope("send_sums"):
                 for o in SIDES[parity]:
                     to = partner(o)
-                    start = pl.multiple_of(to[0] * 64 + first, 16)
                     send(
-                        sums.at[parity, places_of[o[2]][o[0]], pl.ds(start, size)],
+                        sums.at[parity, pl.ds(first, size), places_of[o[2]][o[0]], to[0]],
                         mixed.at[mine, pl.ds(first, size)],
                         index,
                         to,
                     )
-    mixed[mine] = sums[0, slot, pl.ds(row, 64)]
+    for quarter in range(4):
+        mixed[mine, quarter] = sums[0, quarter, slot, pr]
 
     def finish(at, carry):
         start = at * 16 if isinstance(at, int) else pl.multiple_of(at * 16, 16)
@@ -252,12 +263,12 @@
         def turn(group, carry):
             channel = pl.multiple_of(group * 8, 8)
             stage[:, pl.ds(channel, 8), :] = jnp.swapaxes(
-                mixed[pl.ds(channel, 8), pl.ds(start, 16), :].astype(jnp.float32), 0, 1
+                mixed[pl.ds(channel, 8), at].astype(jnp.float32), 0, 1
             )
             return carry
 
         with jax.named_scope("turn"):
-            lax.fori_loop(0, 16, turn, 0)
+            lax.fori_loop(0, 16, turn, 0, unroll=8)
 
         def line(inner, carry):
             values = stage[inner]
@@ -274,18 +285,16 @@
             return carry
 
         with jax.named_scope("line"):
-            lax.fori_loop(0, 16, line, 0, unroll=4)
+            lax.fori_loop(0, 16, line, 0, unroll=16)
         return carry
 
     with jax.named_scope("wait_sums"):
         settle(mixed.at[pl.ds(0, 63)], recv_sem.at[4])
-        settle(mixed.at[pl.ds(0, 48)], recv_sem.at[5])
-    with jax.named_scope("finish_a"):
-        lax.fori_loop(0, 3, finish, 0)
-    with jax.named_scope("wait_last"):
-        settle(mixed.at[pl.ds(0, 16)], recv_sem.at[6])
-    with jax.named_scope("finish_b"):
-        finish(3, 0)
+    for first, size, index in PIECES[1]:
+        with jax.named_scope("wait_piece"):
+            settle(mixed.at[pl.ds(0, 16 * size)], recv_sem.at[index])
+        with jax.named_scope("finish"):
+            lax.fori_loop(first, first + size, finish, 0)
 
     with jax.named_scope("drain"):
         settle(left_send.at[0, pl.ds(0, 127)], send_sem.at[0])
@@ -293,8 +302,8 @@
         settle(strips.at[0, pl.ds(0, 1008)], send_sem.at[2])
         settle(strips.at[1], send_sem.at[3])
         settle(mixed.at[pl.ds(0, 63)], send_sem.at[4])
-        settle(mixed.at[pl.ds(0, 48)], send_sem.at[5])
-        settle(mixed.at[pl.ds(0, 16)], send_sem.at[6])
+        for _, size, index in PIECES[1]:
+            settle(mixed.at[pl.ds(0, 16 * size)], send_sem.at[index])
 
 
 def on_device(
@@ -316,13 +325,14 @@
             pltpu.VMEM((2, 128, 32, 128), half),
             pltpu.VMEM((128, 64, 128), half),
             pltpu.VMEM((1024, 1024), half),
+            pltpu.VMEM((4, 16, 16, 1024), half),
             pltpu.VMEM((2, 1024, 512), half),
-            pltpu.VMEM((2, 4, 1024, 128), half),
-            pltpu.VMEM((128, 64, 128), half),
+            pltpu.VMEM((2, 4, 4, 16, 16, 128), half),
+            pltpu.VMEM((128, 4, 16, 128), half),
             pltpu.VMEM((64, 128, 128), single),
             pltpu.SemaphoreType.DMA((9,)),
-            pltpu.SemaphoreType.DMA((7,)),
-            pltpu.SemaphoreType.DMA((7,)),
+            pltpu.SemaphoreType.DMA((8,)),
+            pltpu.SemaphoreType.DMA((8,)),
         ],
         compiler_params=pltpu.CompilerParams(
             collective_id=0, has_side_effects=True, vmem_limit_bytes=50 * 1024 * 1024

time: 86.3 us -> 83.6 us (0.969)
  Pallas kernels: 84.5 us -> 82.1 us
    pallas_call x1, Pallas kernels: 84.5 us -> 82.1 us  [on_device(): call(*(pltpu.with_memory_space_constraint(a, pltpu.HBM) for a in operands))]
where the time goes in v5:
time: 83.6 us; the launch traced here: 83.4 us
  Pallas kernels  82.1 us (98%)
  local copies, waits for them, and re-layouts  1.32 us (2%)
    pallas_call x1, Pallas kernels, on_device(): call(*(pltpu.with_memory_space_constraint(a, pltpu.HBM) for a in operands))  82.1 us

profile of v5, /device:TPU:1, one launch (start us, length us, event | category | flops | bytes accessed | tf_op | source)
XLA Modules:
  0.0 83.4 jit_solution(14583089475242512203)
XLA Ops:
  0.0 82.1 %triangle.1 = bf16[64,128,128]{2,1,0:T(8,128)(2,1)S(1)} custom-call(bf16[64,128,128]{2,1,0:T(8,128)(2,1)} %pair_hbm.1, bf16[128,128]{1,0:T(8,128)(2,1)} %left_weight_hbm.1, bf16[128,128]{1,0:T(8,128)(2,1)} %right_weight_hbm.1, bf16[128,128]{1,0:T(8,128)(2,1)} %left_gate_hbm.1, bf16[128,128]{1,0:T(8,128)(2,1)} %right_gate_hbm.1, f32[1,128]{1,0:T(1,128)} %bitcast.1, ...), custom_call_target="tpu_custom_call" | custom-call | tf_op jit(solution)/shard_map/triangle/pallas_call | solution.py:352
  82.1 1.3 %copy.10 = bf16[64,128,128]{2,1,0:T(8,128)(2,1)} copy(bf16[64,128,128]{2,1,0:T(8,128)(2,1)S(1)} %triangle.1) | data formatting | bytes 4194304

commit v6 on v5

--- a/solution.py
+++ b/solution.py
@@ -38,6 +38,40 @@
 SIDES = [[o for o in ORDER if o[0] % 2 == parity] for parity in (0, 1)]
 
 
+def finish_rows(at, mixed_rows, gate_rows, out_weight, gains, stage, out_rows):
+    def turn(group, carry):
+        channel = pl.multiple_of(group * 8, 8)
+        stage[:, pl.ds(channel, 8), :] = jnp.swapaxes(
+            mixed_rows[pl.ds(channel, 8)].astype(jnp.float32), 0, 1
+        )
+        return carry
+
+    lax.fori_loop(0, 16, turn, 0, unroll=8)
+
+    def line(inner, carry):
+        values = stage[inner]
+        centred = values - jnp.mean(values, axis=0, keepdims=True)
+        spread = lax.rsqrt(jnp.mean(centred * centred, axis=0, keepdims=True) + 1e-05)
+        scaled = (centred * spread * gains[...]).astype(jnp.bfloat16)
+        product = lax.dot_general(
+            scaled, out_weight[...], (((0,), (0,)), ((), ())), preferred_element_type=jnp.float32
+        )
+        out_rows[at + inner] = (product * gate_rows[at + inner]).astype(jnp.bfloat16)
+        return carry
+
+    lax.fori_loop(0, 16, line, 0, unroll=16)
+
+
+def last_kernel(rows_ref, mixed, gate, out_weight, gains, out_hbm, stage, last, sems):
+    first = pltpu.make_async_copy(rows_ref, out_hbm.at[pl.ds(0, 48)], sems.at[0])
+    first.start()
+    finish_rows(0, mixed.at[:, 3], gate.at[pl.ds(48, 16)], out_weight, gains, stage, last)
+    second = pltpu.make_async_copy(last, out_hbm.at[pl.ds(48, 16)], sems.at[1])
+    second.start()
+    first.wait()
+    second.wait()
+
+
 def triangle_kernel(
     scale,
     pair_hbm,
@@ -49,11 +83,14 @@
     out_weight_hbm,
     out_gate_hbm,
     out_ref,
+    mixed,
+    gate,
+    weight_ref,
+    gains,
     pair,
     weights,
     gain_row,
     turned,
-    gains,
     stage,
     left_send,
     right_send,
@@ -61,8 +98,6 @@
     lines_t,
     strips,
     sums,
-    mixed,
-    gate,
     load_sem,
     send_sem,
     recv_sem,
@@ -258,34 +293,8 @@
         mixed[mine, quarter] = sums[0, quarter, slot, pr]
 
     def finish(at, carry):
-        start = at * 16 if isinstance(at, int) else pl.multiple_of(at * 16, 16)
-
-        def turn(group, carry):
-            channel = pl.multiple_of(group * 8, 8)
-            stage[:, pl.ds(channel, 8), :] = jnp.swapaxes(
-                mixed[pl.ds(channel, 8), at].astype(jnp.float32), 0, 1
-            )
-            return carry
-
-        with jax.named_scope("turn"):
-            lax.fori_loop(0, 16, turn, 0, unroll=8)
-
-        def line(inner, carry):
-            values = stage[inner]
-            centred = values - jnp.mean(values, axis=0, keepdims=True)
-            spread = lax.rsqrt(jnp.mean(centred * centred, axis=0, keepdims=True) + 1e-05)
-            scaled = (centred * spread * gains[...]).astype(jnp.bfloat16)
-            product = lax.dot_general(
-                scaled,
-                weights[4],
-                (((0,), (0,)), ((), ())),
-                preferred_element_type=jnp.float32,
-            )
-            out_ref[start + inner] = (product * gate[start + inner]).astype(jnp.bfloat16)
-            return carry
-
-        with jax.named_scope("line"):
-            lax.fori_loop(0, 16, line, 0, unroll=16)
+        start = pl.multiple_of(at * 16, 16)
+        finish_rows(start, mixed.at[:, at], gate, weights.at[4], gains, stage, out_ref)
         return carry
 
     with jax.named_scope("wait_sums"):
@@ -293,8 +302,10 @@
     for first, size, index in PIECES[1]:
         with jax.named_scope("wait_piece"):
             settle(mixed.at[pl.ds(0, 16 * size)], recv_sem.at[index])
-        with jax.named_scope("finish"):
-            lax.fori_loop(first, first + size, finish, 0)
+        if first < 3:
+            with jax.named_scope("finish"):
+                lax.fori_loop(first, first + size, finish, 0)
+    weight_ref[...] = weights[4]
 
     with jax.named_scope("drain"):
         settle(left_send.at[0, pl.ds(0, 127)], send_sem.at[0])
@@ -312,15 +323,20 @@
     half, single = jnp.bfloat16, jnp.float32
     call = pl.pallas_call(
         functools.partial(triangle_kernel, 1024 ** (-0.5)),
-        out_shape=jax.ShapeDtypeStruct(pair_array.shape, half),
+        out_shape=(
+            jax.ShapeDtypeStruct((48, 128, 128), half),
+            jax.ShapeDtypeStruct((128, 4, 16, 128), half),
+            jax.ShapeDtypeStruct((64, 128, 128), single),
+            jax.ShapeDtypeStruct((128, 128), half),
+            jax.ShapeDtypeStruct((128, 128), single),
+        ),
         in_specs=[pl.BlockSpec(memory_space=pltpu.HBM)] * 8,
-        out_specs=pl.BlockSpec(memory_space=pltpu.VMEM),
+        out_specs=[pl.BlockSpec(memory_space=pltpu.VMEM)] * 5,
         scratch_shapes=[
             pltpu.VMEM((64, 128, 128), half),
             pltpu.VMEM((6, 128, 128), half),
             pltpu.VMEM((1, 128), single),
             pltpu.VMEM((4, 128, 128), half),
-            pltpu.VMEM((128, 128), single),
             pltpu.VMEM((16, 128, 128), single),
             pltpu.VMEM((2, 128, 32, 128), half),
             pltpu.VMEM((128, 64, 128), half),
@@ -328,14 +344,12 @@
             pltpu.VMEM((4, 16, 16, 1024), half),
             pltpu.VMEM((2, 1024, 512), half),
             pltpu.VMEM((2, 4, 4, 16, 16, 128), half),
-            pltpu.VMEM((128, 4, 16, 128), half),
-            pltpu.VMEM((64, 128, 128), single),
             pltpu.SemaphoreType.DMA((9,)),
             pltpu.SemaphoreType.DMA((8,)),
             pltpu.SemaphoreType.DMA((8,)),
         ],
         compiler_params=pltpu.CompilerParams(
-            collective_id=0, has_side_effects=True, vmem_limit_bytes=50 * 1024 * 1024
+            collective_id=0, has_side_effects=True, vmem_limit_bytes=40 * 1024 * 1024
         ),
         name="triangle",
     )
@@ -349,7 +363,20 @@
         out_weight,
         out_gate,
     )
-    return call(*(pltpu.with_memory_space_constraint(a, pltpu.HBM) for a in operands))
+    parts = call(*(pltpu.with_memory_space_constraint(a, pltpu.HBM) for a in operands))
+    return pl.pallas_call(
+        last_kernel,
+        out_shape=jax.ShapeDtypeStruct(pair_array.shape, half),
+        in_specs=[pl.BlockSpec(memory_space=pltpu.VMEM)] * 5,
+        out_specs=pl.BlockSpec(memory_space=pltpu.HBM),
+        scratch_shapes=[
+            pltpu.VMEM((16, 128, 128), single),
+            pltpu.VMEM((16, 128, 128), half),
+            pltpu.SemaphoreType.DMA((2,)),
+        ],
+        compiler_params=pltpu.CompilerParams(vmem_limit_bytes=16 * 1024 * 1024),
+        name="last_rows",
+    )(*parts)
 
 
 def solution(mesh):

time: 83.6 us -> 83.1 us (level)
  local copies, waits for them, and re-layouts: 1.32 us -> 0 us
    pallas_call x0 -> x1, Pallas kernels: none -> 1.54 us  [on_device(): pl.pallas_call(last_kernel, out_shape=jax.ShapeDtypeStruct(pair_array.sha...]
    unnamed x1 -> x0, local copies, waits for them, and re-layouts: 1.32 us -> none
where the time goes in v6:
time: 83.1 us; the launch traced here: 82.9 us
  Pallas kernels  82.9 us (100%)
    pallas_call x1, Pallas kernels, on_device(): call(*(pltpu.with_memory_space_constraint(a, pltpu.HBM) for a in operands))  81.4 us

profile of v6, /device:TPU:1, one launch (start us, length us, event | category | flops | bytes accessed | tf_op | source)
XLA Modules:
  0.0 82.9 jit_solution(9738705230386213074)
XLA Ops:
  0.0 81.4 %triangle.1 = (bf16[48,128,128]{2,1,0:T(8,128)(2,1)S(1)}, bf16[128,4,16,128]{3,2,1,0:T(8,128)(2,1)S(1)}, f32[64,128,128]{2,1,0:T(8,128)S(1)}, bf16[128,128]{1,0:T(8,128)(2,1)S(1)}, f32[128,128]{1,0:T(8,128)S(1)}) custom-call(bf16[64,128,128]{2,1,0:T(8,128)(2,1)} %pair_hbm.1, bf16[128,128]{1,0:T(8,128)(2,1)} %left_weight_hbm.1, ...), custom_call_target="tpu_custom_call" | custom-call | tf_op jit(solution)/shard_map/triangle/pallas_call | solution.py:366
  81.4 1.5 %last_rows.1 = bf16[64,128,128]{2,1,0:T(8,128)(2,1)} custom-call(bf16[48,128,128]{2,1,0:T(8,128)(2,1)S(1)} %get-tuple-element.10.rows_ref, bf16[128,4,16,128]{3,2,1,0:T(8,128)(2,1)S(1)} %get-tuple-element.11.mixed, f32[64,128,128]{2,1,0:T(8,128)S(1)} %get-tuple-element.12.gate, bf16[128,128]{1,0:T(8,128)(2,1)S(1)} %get-tuple-element.13.out_weight, ...), custom_call_target="tpu_custom_call" | custom-call | tf_op jit(solution)/shard_map/last_rows/pallas_call | solution.py:367
